TPU v7x, 32 devices: a whole 2x2x4 slice. The times are simulated.
32 devices in a mesh: dp: 4 (over y, x), row: 2 (over core), col: 4 (over z).
Axes of the slice: x: 2, y: 2, z: 4, core: 2. Of those that a mesh axis runs over, the one named last changes fastest.
Arguments:
- tokens: bfloat16 [4096, 2048], P('dp', ('row', 'col')), may hold values from -40 to 40
- gain_attn: float32 [2048], P(('row', 'col')), may hold values from 0.5 to 1.5
- gain_ffn: float32 [2048], P(('row', 'col')), may hold values from 0.5 to 1.5
- w_query: bfloat16 [2048, 2048], P('row', 'col'), may hold values from -0.125 to 0.125
- w_key: bfloat16 [2048, 2048], P('row', 'col'), may hold values from -0.125 to 0.125
- w_value: bfloat16 [2048, 2048], P('row', 'col'), may hold values from -0.125 to 0.125
- w_out: bfloat16 [2048, 2048], P('col', 'row'), may hold values from -1 to 1
- w_gate: bfloat16 [2048, 8192], P('row', 'col'), may hold values from -0.125 to 0.125
- w_up: bfloat16 [2048, 8192], P('row', 'col'), may hold values from -0.125 to 0.125
- w_down: bfloat16 [8192, 2048], P('col', 'row'), may hold values from -0.0625 to 0.0625
- grad_output: bfloat16 [4096, 2048], P('dp', ('row', 'col')), may hold values from -6 to 6
- segments: int32 [4, 1024], P('dp'), may hold values from 0 to 2, as said below
- positions: int32 [4, 1024], P('dp'), may hold values from 0 to 2047, as said below
Outputs:
- output: float32 [4096, 2048], P('dp', ('row', 'col'))
- grad_tokens: float32 [4096, 2048], P('dp', ('row', 'col'))
- grad_gain_attn: float32 [8, 4, 64], P(('row', 'col'), 'dp')
- grad_gain_ffn: float32 [8, 4, 64], P(('row', 'col'), 'dp')
- grad_w_query: float32 [2, 4, 256, 2048], P('row', 'dp', None, 'col')
- grad_w_key: float32 [2, 4, 256, 2048], P('row', 'dp', None, 'col')
- grad_w_value: float32 [2, 4, 256, 2048], P('row', 'dp', None, 'col')
- grad_w_out: float32 [4, 4, 128, 2048], P('col', 'dp', None, 'row')
- grad_w_gate: float32 [2, 4, 256, 8192], P('row', 'dp', None, 'col')
- grad_w_up: float32 [2, 4, 256, 8192], P('row', 'dp', None, 'col')
- grad_w_down: float32 [4, 4, 512, 2048], P('col', 'dp', None, 'row')
Inputs may be any that keep to these rules, and one draw needn't show every extreme that they name: `segments`: within a sequence the numbers never fall; each sequence holds three documents. `positions`: positions count up by one inside a document; the first document of a sequence starts at a position no larger than 2048 minus its length, the others at 0.
All inputs are finite; a program needn't handle non-finite values.
Results may differ from a plain program's by a relative error of at most 0.015.
Values may be sent and summed in bfloat16 or wider, within the bound.
A program may use at most 256 MiB of HBM per device.

v0:
```python
import jax
import jax.numpy as jnp
from jax import lax
from jax.sharding import PartitionSpec as P

D = 2048
HD = 64


norm_eps = 1e-05
rope_base = 130000.0
masked_score = -1e30


def width_total(partial_sums):
    return lax.psum(partial_sums, ("row", "col"))


def gather_cols(pieces):
    return lax.all_gather(pieces, "col", axis=1, tiled=True)


def sum_cols(partial_sums):
    return lax.psum_scatter(partial_sums, "col", scatter_dimension=1, tiled=True)


def gather_rows(pieces):
    return lax.all_gather(pieces, "row", axis=2, tiled=True)


def sum_rows(partial_sums):
    return lax.psum_scatter(partial_sums, "row", scatter_dimension=2, tiled=True)


def product(left, right):
    return jnp.dot(left, right, preferred_element_type=jnp.float32)


def contract_rows(left, right):
    return jnp.einsum("ta,tb->ab", left, right, preferred_element_type=jnp.float32)


def times_transposed(left, right):
    return jnp.einsum("ta,ba->tb", left, right, preferred_element_type=jnp.float32)


def norm_forward(residual, gain_vec):
    squares = width_total(jnp.sum(residual * residual, axis=1))
    scale_inv = lax.rsqrt(squares / D + norm_eps)
    normed = residual * scale_inv[:, None]
    return (normed, scale_inv, (normed * gain_vec).astype(jnp.bfloat16))


def norm_backward(grad_normed_out, normed, scale_inv, gain_vec):
    grad_normed = grad_normed_out * gain_vec
    inner_sum = width_total(jnp.sum(grad_normed * normed, axis=1))
    grad_input = scale_inv[:, None] * (grad_normed - normed * (inner_sum / D)[:, None])
    return (grad_input, jnp.sum(grad_normed_out * normed, axis=0))


def rope_tables(positions):
    half_steps = jnp.arange(HD // 2, dtype=jnp.float32)
    inv_freq = rope_base ** (-2.0 * half_steps / HD)
    angles = positions.astype(jnp.float32)[:, None] * inv_freq[None, :]
    return (jnp.cos(angles)[:, None, :], jnp.sin(angles)[:, None, :])


def rotate(values, cos_table, sin_table):
    half_dim = values.shape[-1] // 2
    first_half = values[..., :half_dim]
    second_half = values[..., half_dim:]
    return jnp.concatenate(
        [
            first_half * cos_table - second_half * sin_table,
            second_half * cos_table + first_half * sin_table,
        ],
        axis=-1,
    )


def unrotate(values, cos_table, sin_table):
    half_dim = values.shape[-1] // 2
    first_half = values[..., :half_dim]
    second_half = values[..., half_dim:]
    return jnp.concatenate(
        [
            first_half * cos_table + second_half * sin_table,
            second_half * cos_table - first_half * sin_table,
        ],
        axis=-1,
    )


def score_rows(query_part, key_rows, segment, row_start):
    row_count = query_part.shape[0]
    seq_len = key_rows.shape[0]
    scores = jnp.einsum(
        "qhd,khd->hqk", query_part, key_rows, preferred_element_type=jnp.float32
    ) * key_rows.shape[2] ** (-0.5)
    query_slot = row_start + jnp.arange(row_count)
    key_slot = jnp.arange(seq_len)
    query_seg = segment[row_start : row_start + row_count]
    allowed = (key_slot[None, :] <= query_slot[:, None]) & (query_seg[:, None] == segment[None, :])
    return jnp.where(allowed[None], scores, masked_score)


def attend_forward(inputs):
    queries, key_rows, value_rows, segment = inputs
    seq_len = queries.shape[0]
    span = min(512, seq_len)
    results = []
    log_parts = []
    for row_start in range(0, seq_len, span):
        scores = score_rows(queries[row_start : row_start + span], key_rows, segment, row_start)
        log_total = jnp.log(jnp.sum(jnp.exp(scores), axis=-1))
        attn_probs = jnp.exp(scores - log_total[..., None]).astype(jnp.bfloat16)
        results.append(
            jnp.einsum("hqk,khd->qhd", attn_probs, value_rows, preferred_element_type=jnp.float32)
        )
        log_parts.append(log_total)
    return (jnp.concatenate(results, axis=0), jnp.concatenate(log_parts, axis=1))


def attend_backward(inputs):
    queries, key_rows, value_rows, segment, log_totals, grad_rows = inputs
    seq_len = queries.shape[0]
    span = min(512, seq_len)
    score_scale = queries.shape[2] ** (-0.5)
    grad_query_parts = []
    grad_keys = jnp.zeros(key_rows.shape, jnp.float32)
    grad_values = jnp.zeros(value_rows.shape, jnp.float32)
    for row_start in range(0, seq_len, span):
        query_part = queries[row_start : row_start + span]
        grad_part = grad_rows[row_start : row_start + span]
        scores = score_rows(query_part, key_rows, segment, row_start)
        attn_probs = jnp.exp(scores - log_totals[:, row_start : row_start + span, None])
        grad_probs = jnp.einsum(
            "qhd,khd->hqk", grad_part, value_rows, preferred_element_type=jnp.float32
        )
        weighted = jnp.sum(attn_probs * grad_probs, axis=-1, keepdims=True)
        grad_scores = (attn_probs * (grad_probs - weighted) * score_scale).astype(jnp.bfloat16)
        grad_query_parts.append(
            jnp.einsum("hqk,khd->qhd", grad_scores, key_rows, preferred_element_type=jnp.float32)
        )
        grad_keys = grad_keys + jnp.einsum(
            "hqk,qhd->khd", grad_scores, query_part, preferred_element_type=jnp.float32
        )
        grad_values = grad_values + jnp.einsum(
            "hqk,qhd->khd",
            attn_probs.astype(jnp.bfloat16),
            grad_part,
            preferred_element_type=jnp.float32,
        )
    return (jnp.concatenate(grad_query_parts, axis=0), grad_keys, grad_values)


def as_blocks(matrix):
    return matrix.reshape((1, 1) + matrix.shape)


def body(
    tokens,
    gain_attn,
    gain_ffn,
    w_query,
    w_key,
    w_value,
    w_out,
    w_gate,
    w_up,
    w_down,
    grad_output,
    segments,
    positions,
):
    residual = tokens.astype(jnp.float32)
    tok_count = residual.shape[0]
    seq_count, seq_len = segments.shape
    cos_table, sin_table = rope_tables(positions.reshape(tok_count))
    normed_one, inv_one, hidden_one = norm_forward(residual, gain_attn)
    gathered_one = gather_cols(hidden_one)
    projected = jnp.stack(
        [
            product(gathered_one, w_query),
            product(gathered_one, w_key),
            product(gathered_one, w_value),
        ]
    )
    local_qkv = sum_rows(projected)
    head_shape = (seq_count, seq_len, local_qkv.shape[2] // HD, HD)
    flat_heads = (tok_count, local_qkv.shape[2] // HD, HD)
    queries = (
        rotate(local_qkv[0].reshape(flat_heads), cos_table, sin_table)
        .astype(jnp.bfloat16)
        .reshape(head_shape)
    )
    key_rows = (
        rotate(local_qkv[1].reshape(flat_heads), cos_table, sin_table)
        .astype(jnp.bfloat16)
        .reshape(head_shape)
    )
    value_rows = local_qkv[2].astype(jnp.bfloat16).reshape(head_shape)
    attended, log_totals = lax.map(attend_forward, (queries, key_rows, value_rows, segments))
    heads_out = attended.reshape(tok_count, -1).astype(jnp.bfloat16)
    heads_all = gather_rows(heads_out[None])[0]
    middle = residual + sum_cols(product(heads_all, w_out))
    normed_two, inv_two, hidden_two = norm_forward(middle, gain_ffn)
    gathered_two = gather_cols(hidden_two)
    gate_up = sum_rows(jnp.stack([product(gathered_two, w_gate), product(gathered_two, w_up)]))
    gate_pre = gate_up[0]
    up_pre = gate_up[1]
    gate_sigmoid = jax.nn.sigmoid(gate_pre)
    hidden_units = (gate_pre * gate_sigmoid * up_pre).astype(jnp.bfloat16)
    units_all = gather_rows(hidden_units[None])[0]
    output = middle + sum_cols(product(units_all, w_down))
    grad_all = gather_cols(grad_output)
    units_all = gather_rows(hidden_units[None])[0]
    grad_w_down = contract_rows(units_all, grad_all)
    grad_units = sum_rows(times_transposed(grad_all, w_down)[None])[0]
    grad_gate = (
        grad_units * up_pre * gate_sigmoid * (1.0 + gate_pre * (1.0 - gate_sigmoid))
    ).astype(jnp.bfloat16)
    grad_up = (grad_units * gate_pre * gate_sigmoid).astype(jnp.bfloat16)
    gathered_two = gather_cols(hidden_two)
    grad_pair = gather_rows(jnp.stack([grad_gate, grad_up]))
    grad_w_gate = contract_rows(gathered_two, grad_pair[0])
    grad_w_up = contract_rows(gathered_two, grad_pair[1])
    grad_two = sum_cols(
        times_transposed(grad_pair[0], w_gate) + times_transposed(grad_pair[1], w_up)
    )
    grad_norm_two, grad_gain_ffn = norm_backward(grad_two, normed_two, inv_two, gain_ffn)
    grad_middle = grad_output.astype(jnp.float32) + grad_norm_two
    grad_branch = gather_cols(grad_middle.astype(jnp.bfloat16))
    heads_all = gather_rows(heads_out[None])[0]
    grad_w_out = contract_rows(heads_all, grad_branch)
    grad_heads = sum_rows(times_transposed(grad_branch, w_out)[None])[0].astype(jnp.bfloat16)
    grad_queries, grad_keys, grad_values = lax.map(
        attend_backward,
        (queries, key_rows, value_rows, segments, log_totals, grad_heads.reshape(head_shape)),
    )
    grad_query_pre = (
        unrotate(grad_queries.reshape(flat_heads), cos_table, sin_table)
        .reshape(tok_count, -1)
        .astype(jnp.bfloat16)
    )
    grad_key_pre = (
        unrotate(grad_keys.reshape(flat_heads), cos_table, sin_table)
        .reshape(tok_count, -1)
        .astype(jnp.bfloat16)
    )
    grad_value_pre = grad_values.reshape(tok_count, -1).astype(jnp.bfloat16)
    grad_triple = gather_rows(jnp.stack([grad_query_pre, grad_key_pre, grad_value_pre]))
    gathered_one = gather_cols(hidden_one)
    grad_w_query = contract_rows(gathered_one, grad_triple[0])
    grad_w_key = contract_rows(gathered_one, grad_triple[1])
    grad_w_value = contract_rows(gathered_one, grad_triple[2])
    grad_one = sum_cols(
        times_transposed(grad_triple[0], w_query)
        + times_transposed(grad_triple[1], w_key)
        + times_transposed(grad_triple[2], w_value)
    )
    grad_norm_one, grad_gain_attn = norm_backward(grad_one, normed_one, inv_one, gain_attn)
    grad_tokens = grad_middle + grad_norm_one
    reduced = (
        lax.psum_scatter(grad_gain_attn, "dp", scatter_dimension=0, tiled=True),
        lax.psum_scatter(grad_gain_ffn, "dp", scatter_dimension=0, tiled=True),
        lax.psum_scatter(grad_w_query, "dp", scatter_dimension=0, tiled=True),
        lax.psum_scatter(grad_w_key, "dp", scatter_dimension=0, tiled=True),
        lax.psum_scatter(grad_w_value, "dp", scatter_dimension=0, tiled=True),
        lax.psum_scatter(grad_w_out, "dp", scatter_dimension=0, tiled=True),
        lax.psum_scatter(grad_w_gate, "dp", scatter_dimension=0, tiled=True),
        lax.psum_scatter(grad_w_up, "dp", scatter_dimension=0, tiled=True),
        lax.psum_scatter(grad_w_down, "dp", scatter_dimension=0, tiled=True),
    )
    gate_share, up_share = (reduced[6], reduced[7])
    return (
        output,
        grad_tokens,
        as_blocks(reduced[0]),
        as_blocks(reduced[1]),
        as_blocks(reduced[2]),
        as_blocks(reduced[3]),
        as_blocks(reduced[4]),
        as_blocks(reduced[5]),
        as_blocks(gate_share),
        as_blocks(up_share),
        as_blocks(reduced[8]),
    )


def solution(mesh):
    return jax.shard_map(
        body,
        mesh=mesh,
        in_specs=(
            P("dp", ("row", "col")),
            P(("row", "col")),
            P(("row", "col")),
            P("row", "col"),
            P("row", "col"),
            P("row", "col"),
            P("col", "row"),
            P("row", "col"),
            P("row", "col"),
            P("col", "row"),
            P("dp", ("row", "col")),
            P("dp", None),
            P("dp", None),
        ),
        out_specs=(
            P("dp", ("row", "col")),
            P("dp", ("row", "col")),
            P(("row", "col"), "dp", None),
            P(("row", "col"), "dp", None),
            P("row", "dp", None, "col"),
            P("row", "dp", None, "col"),
            P("row", "dp", None, "col"),
            P("col", "dp", None, "row"),
            P("row", "dp", None, "col"),
            P("row", "dp", None, "col"),
            P("col", "dp", None, "row"),
        ),
        check_vma=False,
    )
```

profile of v0, /device:TPU:0, one launch (start us, length us, event | category | flops | bytes accessed | tf_op | source)
XLA Modules:
  0.0 1258.7 jit_solution(7421168657881235583)
XLA Ops:
  8.6 18.5 %psum.28 = f32[1024]{0:T(1024)S(1)} all-reduce(f32[1024]{0:T(1024)S(1)} %fusion.95), channel_id=1, replica_groups=mesh['dp'=4,'row'=2,'col'=4] {'row','col'}, use_global_device_ids=true, to_apply=%region_1.0 | all-reduce | flops 1024 | bytes 8192 | tf_op jit(solution)/shard_map/psum | solution.py:16
  29.3 44.6 %all-gather.9.cloned.1.call-done = bf16[1024,1024]{1,0:T(8,128)(2,1)} async-done(((bf16[1024,256]{1,0:T(8,128)(2,1)}), bf16[1024,1024]{1,0:T(8,128)(2,1)}) %all-gather.9.cloned.1.call-update) | async-done | bytes 2097168 | tf_op jit(solution)/shard_map/all_gather | solution.py:20
  73.9 3.2 convolution_bitcast_fusion.4
  79.7 3.4 pad_maximum_fusion.1
  86.2 9.0 reduce-scatter.16.cloned.1.call-done
  95.2 2.6 fusion.129
  102.2 2.5 subtract_convert_fusion.2
  104.7 8.7 fusion.5
  113.5 7.0 fusion.4
  120.5 4.9 fusion.86
  128.6 10.4 all-gather.11.cloned.1.call-done
  139.0 4.4 fusion.98
  144.1 77.5 %reduce-scatter.18.cloned.1.call-done = f32[1024,256]{1,0:T(8,128)} async-done(((f32[1024,1024]{1,0:T(8,128)}), f32[1024,256]{1,0:T(8,128)}) %reduce-scatter.18.cloned.1.call-update) | async-done | bytes 1048592 | tf_op jit(solution)/shard_map/reduce_scatter | solution.py:24
  223.1 16.6 %psum.29 = f32[1024]{0:T(1024)S(1)} all-reduce(f32[1024]{0:T(1024)S(1)} %get-tuple-element.68), channel_id=1, replica_groups=mesh['dp'=4,'row'=2,'col'=4] {'row','col'}, use_global_device_ids=true, to_apply=%region_7.8 | all-reduce | flops 1024 | bytes 8192 | tf_op jit(solution)/shard_map/psum | solution.py:16
  240.9 29.1 %all-gather.17.cloned.1.call-done = bf16[1024,1024]{1,0:T(8,128)(2,1)} async-done(((bf16[1024,256]{1,0:T(8,128)(2,1)}), bf16[1024,1024]{1,0:T(8,128)(2,1)}) %all-gather.17.cloned.1.call-update) | async-done | bytes 2097168 | tf_op jit(solution)/shard_map/all_gather | solution.py:20
  270.1 10.6 convolution_bitcast_fusion
  280.7 35.8 %all-gather.13.cloned.1.call-done = bf16[1024,1024]{1,0:T(8,128)(2,1)} async-done(((bf16[1024,256]{1,0:T(8,128)(2,1)}), bf16[1024,1024]{1,0:T(8,128)(2,1)}) %all-gather.13.cloned.1.call-update) | async-done | bytes 2097168 | tf_op jit(solution)/shard_map/all_gather | solution.py:20
  316.5 7.1 convolution_bitcast_fusion.1
  323.6 4.5 convolution_bitcast_fusion.2
  328.1 7.0 pad_maximum_fusion
  335.3 26.6 %reduce-scatter.20.cloned.1.call-done = f32[2,1024,1024]{2,1,0:T(8,128)} async-done(((f32[2,1024,2048]{2,1,0:T(8,128)}), f32[2,1024,1024]{2,1,0:T(8,128)}) %reduce-scatter.20.cloned.1.call-update) | async-done | bytes 8388624 | tf_op jit(solution)/shard_map/reduce_scatter | solution.py:32
  361.8 7.0 multiply_convert_fusion.3
  371.4 21.0 %all-gather.19.cloned.1.call-done = bf16[2,1024,2048]{2,1,0:T(8,128)(2,1)} async-done(((bf16[2,1024,1024]{2,1,0:T(8,128)(2,1)}), bf16[2,1024,2048]{2,1,0:T(8,128)(2,1)}) %all-gather.19.cloned.1.call-update) | async-done | bytes 8388624 | tf_op jit(solution)/shard_map/all_gather | solution.py:28
  392.4 7.9 fusion.41
  400.4 6.1 fusion.54
  406.6 78.1 %reduce-scatter.26.cloned.1.call-done = f32[1024,256]{1,0:T(8,128)} async-done(((f32[1024,1024]{1,0:T(8,128)}), f32[1024,256]{1,0:T(8,128)}) %reduce-scatter.26.cloned.1.call-update) | async-done | bytes 1048592 | tf_op jit(solution)/shard_map/reduce_scatter | solution.py:24
  486.3 16.0 %psum.30 = f32[1024]{0:T(1024)S(1)} all-reduce(f32[1024]{0:T(1024)S(1)} %get-tuple-element.53), channel_id=1, replica_groups=mesh['dp'=4,'row'=2,'col'=4] {'row','col'}, use_global_device_ids=true, to_apply=%region_13.14 | all-reduce | flops 1024 | bytes 8192 | tf_op jit(solution)/shard_map/psum | solution.py:16
  502.3 2.4 fusion.123
  504.8 45.1 %all-gather.21.cloned.1.call-done = bf16[1024,1024]{1,0:T(8,128)(2,1)} async-done(((bf16[1024,256]{1,0:T(8,128)(2,1)}), bf16[1024,1024]{1,0:T(8,128)(2,1)}) %all-gather.21.cloned.1.call-update) | async-done | bytes 2097168 | tf_op jit(solution)/shard_map/all_gather | solution.py:20
  549.9 4.2 convolution_bitcast_fusion.3
  554.6 7.5 reduce-scatter.28.cloned.1.call-done
  563.6 4.5 fusion.132
  568.1 12.7 %fusion.29 = f32[4,64,1024]{2,1,0:T(8,128)} fusion(f32[4,512,1024]{2,1,0:T(8,128)} %fusion.5, f32[4,512,1024]{2,1,0:T(8,128)} %fusion.132, bf16[1024,4,32]{0,2,1:T(8,128)(2,1)S(1)} %copy-done.18, bf16[1024,4,32]{0,2,1:T(8,128)(2,1)S(1)} %copy-done.16), kind=kOutput, calls=%fused_computation.43 | convolution fusion | flops 279448576 | bytes 35127296 | tf_op jit(solution)/shard_map/while/body/eval_jaxpr/hqk,qhd->khd/dot_general | solution.py:145
  580.8 13.5 %fusion.74 = f32[512,4,64]{0,2,1:T(8,128)} fusion(f32[4,512,1024]{2,1,0:T(8,128)} %fusion.5, f32[4,512,1024]{2,1,0:T(8,128)} %fusion.132, bf16[1024,4,32]{0,2,1:T(8,128)(2,1)} %get-tuple-element.80, bf16[1024,4,32]{0,2,1:T(8,128)(2,1)S(1)} %copy-done.20), kind=kOutput, calls=%fused_computation.81 | convolution fusion | flops 279972864 | bytes 17825792 | tf_op jit(solution)/shard_map/while/body/eval_jaxpr/hqk,khd->qhd/dot_general | solution.py:143
  595.2 4.5 fusion.133
  599.7 4.3 fusion.44
  604.0 12.0 fusion.71
  616.0 14.0 %fusion.65 = f32[1024,4,64]{0,2,1:T(8,128)} fusion(f32[4,64,1024]{2,1,0:T(8,128)} %fusion.29, f32[4,512,1024]{2,1,0:T(8,128)} %fusion.4, f32[4,512,1024]{2,1,0:T(8,128)} %fusion.133, bf16[1024,4,32]{0,2,1:T(8,128)(2,1)} %get-tuple-element.89, bf16[1024,4,32]{0,2,1:T(8,128)(2,1)} %get-tuple-element.90), kind=kOutput, calls=%fused_computation.78 | convolution fusion | flops 279710720 | bytes 19398656 | tf_op jit(solution)/shard_map/while/body/eval_jaxpr/hqk,qhd->khd/dot_general | solution.py:145
  630.1 4.4 fusion.68
  637.0 12.7 %all-gather.23.cloned.1.call-done = bf16[3,1024,512]{1,2,0:T(8,128)(2,1)} async-done(((bf16[3,1024,256]{1,2,0:T(8,128)(2,1)}), bf16[3,1024,512]{1,2,0:T(8,128)(2,1)}) %all-gather.23.cloned.1.call-update) | async-done | bytes 3145744 | tf_op jit(solution)/shard_map/all_gather | solution.py:28
  649.7 3.0 fusion.105
  652.8 2.6 fusion.107
  655.4 3.4 add_add_fusion
  658.8 7.7 all-gather.15.cloned.1.call-done
  666.6 10.1 fusion.20
  676.8 10.7 fusion.18
  688.7 4.1 fusion.96
  692.9 10.6 fusion.40
  703.6 10.7 fusion.42
  714.4 4.5 fusion.104
  719.3 4.5 fusion.106
  723.8 4.5 fusion.108
  729.7 17.0 %reduce-scatter.30.cloned.1.call-done = f32[1024,256]{1,0:T(8,128)} async-done(((f32[1024,1024]{1,0:T(8,128)}), f32[1024,256]{1,0:T(8,128)}) %reduce-scatter.30.cloned.1.call-update) | async-done | bytes 1048592 | tf_op jit(solution)/shard_map/reduce_scatter | solution.py:24
  748.5 9.8 all-reduce.2
  758.3 16.5 %psum.31 = f32[1024]{0:T(1024)S(1)} all-reduce(f32[1024]{0:T(1024)S(1)} %get-tuple-element.55), channel_id=1, replica_groups=mesh['dp'=4,'row'=2,'col'=4] {'row','col'}, use_global_device_ids=true, to_apply=%region_19.20 | all-reduce | flops 1024 | bytes 8192 | tf_op jit(solution)/shard_map/psum | solution.py:16
  776.0 50.8 %reduce-scatter.22.cloned.1.call-done = f32[1024,256]{1,0:T(8,128)} async-done(((f32[1024,1024]{1,0:T(8,128)}), f32[1024,256]{1,0:T(8,128)}) %reduce-scatter.22.cloned.1.call-update) | async-done | bytes 1048592 | tf_op jit(solution)/shard_map/reduce_scatter | solution.py:24
  826.8 3.2 fusion.93
  830.0 87.1 %reduce-scatter.44.cloned.1.call-done = f32[512,1024]{1,0:T(8,128)} async-done(((f32[2048,1024]{1,0:T(8,128)}), f32[512,1024]{1,0:T(8,128)}) %reduce-scatter.44.cloned.1.call-update) | async-done | bytes 2097168 | tf_op jit(solution)/shard_map/reduce_scatter | solution.py:273
  917.1 38.6 %reduce-scatter.38.cloned.1.call-done = f32[128,1024]{1,0:T(8,128)} async-done(((f32[512,1024]{1,0:T(8,128)}), f32[128,1024]{1,0:T(8,128)}) %reduce-scatter.38.cloned.1.call-update) | async-done | bytes 524304 | tf_op jit(solution)/shard_map/reduce_scatter | solution.py:270
  955.7 90.0 %reduce-scatter.40.cloned.1.call-done = f32[256,2048]{1,0:T(8,128)} async-done(((f32[1024,2048]{1,0:T(8,128)}), f32[256,2048]{1,0:T(8,128)}) %reduce-scatter.40.cloned.1.call-update) | async-done | bytes 2097168 | tf_op jit(solution)/shard_map/reduce_scatter | solution.py:271
  1045.7 89.8 %reduce-scatter.42.cloned.1.call-done = f32[256,2048]{1,0:T(8,128)} async-done(((f32[1024,2048]{1,0:T(8,128)}), f32[256,2048]{1,0:T(8,128)}) %reduce-scatter.42.cloned.1.call-update) | async-done | bytes 2097168 | tf_op jit(solution)/shard_map/reduce_scatter | solution.py:272
  1135.6 38.8 %reduce-scatter.32.cloned.1.call-done = f32[256,512]{1,0:T(8,128)} async-done(((f32[1024,512]{1,0:T(8,128)}), f32[256,512]{1,0:T(8,128)}) %reduce-scatter.32.cloned.1.call-update) | async-done | bytes 524304 | tf_op jit(solution)/shard_map/reduce_scatter | solution.py:267
  1174.3 38.8 %reduce-scatter.34.cloned.1.call-done = f32[256,512]{1,0:T(8,128)} async-done(((f32[1024,512]{1,0:T(8,128)}), f32[256,512]{1,0:T(8,128)}) %reduce-scatter.34.cloned.1.call-update) | async-done | bytes 524304 | tf_op jit(solution)/shard_map/reduce_scatter | solution.py:268
  1213.1 38.8 %reduce-scatter.36.cloned.1.call-done = f32[256,512]{1,0:T(8,128)} async-done(((f32[1024,512]{1,0:T(8,128)}), f32[256,512]{1,0:T(8,128)}) %reduce-scatter.36.cloned.1.call-update) | async-done | bytes 524304 | tf_op jit(solution)/shard_map/reduce_scatter | solution.py:269
  (154 shorter events, 35.1 us)
Async XLA Ops:
  7.2 131.9 %copy-start = (bf16[512,1024]{1,0:T(8,128)(2,1)S(1)}, bf16[512,1024]{1,0:T(8,128)(2,1)}, u32[]{:S(2)}) copy-start(bf16[512,1024]{1,0:T(8,128)(2,1)} %param.19) | copy-start | bytes 3145732
  7.2 66.7 %all-gather.9.cloned.1.call-start = ((), (), s32[]{:S(2)}) async-start(), calls=%async_computation.15 | async-start | bytes 2621440 | tf_op jit(solution)/shard_map/all_gather | solution.py:20
  27.1 50.0 %copy-start.22 = (f32[1024]{0:T(1024)}, f32[1024]{0:T(1024)S(1)}, u32[]{:S(2)}) copy-start(f32[1024]{0:T(1024)S(1)} %add_rsqrt_fusion.1) | copy-start | bytes 12292
  29.2 47.9 %copy-start.34 = (bf16[1024,512]{1,0:T(8,128)(2,1)S(1)}, bf16[1024,512]{1,0:T(8,128)(2,1)}, u32[]{:S(2)}) copy-start(bf16[1024,512]{1,0:T(8,128)(2,1)} %param.17) | copy-start | bytes 3145732
  29.2 66.0 %reduce-scatter.16.cloned.1.call-start = ((), (), s32[]{:S(2)}) async-start(), calls=%async_computation.16 | async-start | bytes 9437184 | tf_op jit(solution)/shard_map/reduce_scatter | solution.py:32
  73.9 3.3 copy-start.31
  77.2 1.3 copy-start.33
  83.0 0.7 copy-start.27
  83.0 0.7 copy-start.25
  83.1 56.0 %all-gather.11.cloned.1.call-start = ((), (), s32[]{:S(2)}) async-start(), calls=%async_computation.17 | async-start | bytes 1572864 | tf_op jit(solution)/shard_map/all_gather | solution.py:28
  84.3 17.9 %copy-start.8 = (f32[1024,32]{0,1:T(8,128)}, f32[1024,32]{0,1:T(8,128)S(1)}, u32[]{:S(2)}) copy-start(f32[1024,32]{0,1:T(8,128)S(1)} %get-tuple-element.92) | copy-start | bytes 393220
  104.7 8.7 copy-start.12
  104.7 8.7 copy-start.15
  104.7 8.7 copy-start.17
  104.7 8.7 copy-start.19
  104.7 8.7 copy-start.21
  120.5 5.8 copy-start.2
  128.6 93.1 %reduce-scatter.18.cloned.1.call-start = ((), (), s32[]{:S(2)}) async-start(), calls=%async_computation.18 | async-start | bytes 5242880 | tf_op jit(solution)/shard_map/reduce_scatter | solution.py:24
  143.5 78.2 %copy-start.3 = (bf16[1024,256]{1,0:T(8,128)(2,1)S(1)}, bf16[1024,256]{1,0:T(8,128)(2,1)}, u32[]{:S(2)}) copy-start(bf16[1024,256]{1,0:T(8,128)(2,1)} %param.13) | copy-start | bytes 1572868
  143.5 96.2 %copy-start.24 = (f32[256]{0:T(256)S(1)}, f32[256]{0:T(256)}, u32[]{:S(2)}) copy-start(f32[256]{0:T(256)} %param.15) | copy-start | bytes 3076
  143.5 126.6 %all-gather.17.cloned.1.call-start = ((), (), s32[]{:S(2)}) async-start(), calls=%async_computation.23 | async-start | bytes 2621440 | tf_op jit(solution)/shard_map/all_gather | solution.py:20
  144.1 172.4 %all-gather.13.cloned.1.call-start = ((), (), s32[]{:S(2)}) async-start(), calls=%async_computation.19 | async-start | bytes 2621440 | tf_op jit(solution)/shard_map/all_gather | solution.py:20
  240.7 94.6 %reduce-scatter.24.cloned.1.call-start = ((), (), s32[]{:S(2)}) async-start(), calls=%async_computation.24 | async-start | bytes 12582912 | tf_op jit(solution)/shard_map/reduce_scatter | solution.py:32
  280.7 81.2 %reduce-scatter.20.cloned.1.call-start = ((), (), s32[]{:S(2)}) async-start(), calls=%async_computation.20 | async-start | bytes 25165824 | tf_op jit(solution)/shard_map/reduce_scatter | solution.py:32
  316.5 7.1 copy-start.29
  316.5 7.1 copy-start.32
  335.2 57.2 %all-gather.19.cloned.1.call-start = ((), (), s32[]{:S(2)}) async-start(), calls=%async_computation.25 | async-start | bytes 12582912 | tf_op jit(solution)/shard_map/all_gather | solution.py:28
  371.1 113.5 %reduce-scatter.26.cloned.1.call-start = ((), (), s32[]{:S(2)}) async-start(), calls=%async_computation.26 | async-start | bytes 5242880 | tf_op jit(solution)/shard_map/reduce_scatter | solution.py:24
  392.4 8.0 copy-start.28
  392.4 8.0 copy-start.30
  406.5 95.8 %copy-start.5 = (bf16[1024,256]{1,0:T(8,128)(2,1)S(1)}, bf16[1024,256]{1,0:T(8,128)(2,1)}, u32[]{:S(2)}) copy-start(bf16[1024,256]{1,0:T(8,128)(2,1)} %param.23) | copy-start | bytes 1572868
  406.6 143.4 %all-gather.21.cloned.1.call-start = ((), (), s32[]{:S(2)}) async-start(), calls=%async_computation.27 | async-start | bytes 2621440 | tf_op jit(solution)/shard_map/all_gather | solution.py:20
  504.7 57.4 %reduce-scatter.28.cloned.1.call-start = ((), (), s32[]{:S(2)}) async-start(), calls=%async_computation.28 | async-start | bytes 3145728 | tf_op jit(solution)/shard_map/reduce_scatter | solution.py:32
  554.1 95.6 %all-gather.23.cloned.1.call-start = ((), (), s32[]{:S(2)}) async-start(), calls=%async_computation.29 | async-start | bytes 4718592 | tf_op jit(solution)/shard_map/all_gather | solution.py:28
  563.6 4.5 copy-start.16
  563.6 4.5 copy-start.18
  568.1 12.7 %copy-start.20 = (bf16[1024,4,32]{0,2,1:T(8,128)(2,1)S(1)}, bf16[1024,4,32]{0,2,1:T(8,128)(2,1)}, u32[]{:S(2)}) copy-start(bf16[1024,4,32]{0,2,1:T(8,128)(2,1)} %get-tuple-element.79) | copy-start | bytes 786436
  594.5 0.7 copy-start.6
  630.1 4.4 copy-start.9
  630.1 4.4 copy-start.11
  630.1 4.4 copy-start.13
  636.2 30.4 %all-gather.15.cloned.1.call-start = ((), (), s32[]{:S(2)}) async-start(), calls=%async_computation.21 | async-start | bytes 6291456 | tf_op jit(solution)/shard_map/all_gather | solution.py:28
  636.8 109.9 %reduce-scatter.30.cloned.1.call-start = ((), (), s32[]{:S(2)}) async-start(), calls=%async_computation.30 | async-start | bytes 5242880 | tf_op jit(solution)/shard_map/reduce_scatter | solution.py:24
  649.7 3.0 copy-start.14
  652.7 2.6 copy-start.10
  658.8 168.0 %reduce-scatter.22.cloned.1.call-start = ((), (), s32[]{:S(2)}) async-start(), calls=%async_computation.22 | async-start | bytes 5242880 | tf_op jit(solution)/shard_map/reduce_scatter | solution.py:24
  676.7 240.4 %reduce-scatter.44.cloned.1.call-start = ((), (), s32[]{:S(2)}) async-start(), calls=%async_computation.37 | async-start | bytes 10485760 | tf_op jit(solution)/shard_map/reduce_scatter | solution.py:273
  687.4 1.2 copy-start.7
  687.5 268.3 %reduce-scatter.38.cloned.1.call-start = ((), (), s32[]{:S(2)}) async-start(), calls=%async_computation.34 | async-start | bytes 2621440 | tf_op jit(solution)/shard_map/reduce_scatter | solution.py:270
  692.8 352.9 %reduce-scatter.40.cloned.1.call-start = ((), (), s32[]{:S(2)}) async-start(), calls=%async_computation.35 | async-start | bytes 10485760 | tf_op jit(solution)/shard_map/reduce_scatter | solution.py:271
  703.6 432.0 %reduce-scatter.42.cloned.1.call-start = ((), (), s32[]{:S(2)}) async-start(), calls=%async_computation.36 | async-start | bytes 10485760 | tf_op jit(solution)/shard_map/reduce_scatter | solution.py:272
  714.4 460.0 %reduce-scatter.32.cloned.1.call-start = ((), (), s32[]{:S(2)}) async-start(), calls=%async_computation.31 | async-start | bytes 2621440 | tf_op jit(solution)/shard_map/reduce_scatter | solution.py:267
  718.9 494.2 %reduce-scatter.34.cloned.1.call-start = ((), (), s32[]{:S(2)}) async-start(), calls=%async_computation.32 | async-start | bytes 2621440 | tf_op jit(solution)/shard_map/reduce_scatter | solution.py:268
  723.7 4.6 copy-start.35
  723.8 23.0 %copy-start.4 = (bf16[1024,256]{1,0:T(8,128)(2,1)S(1)}, bf16[1024,256]{1,0:T(8,128)(2,1)}, u32[]{:S(2)}) copy-start(bf16[1024,256]{1,0:T(8,128)(2,1)} %param.13) | copy-start | bytes 1572868
  723.8 23.0 %copy-start.23 = (f32[1024]{0:T(1024)S(1)}, f32[1024]{0:T(1024)}, u32[]{:S(2)}) copy-start(f32[1024]{0:T(1024)} %copy-done.22) | copy-start | bytes 12292
  723.8 23.0 %copy-start.26 = (f32[256]{0:T(256)S(1)}, f32[256]{0:T(256)}, u32[]{:S(2)}) copy-start(f32[256]{0:T(256)} %param.14) | copy-start | bytes 3076
  723.8 528.1 %reduce-scatter.36.cloned.1.call-start = ((), (), s32[]{:S(2)}) async-start(), calls=%async_computation.33 | async-start | bytes 2621440 | tf_op jit(solution)/shard_map/reduce_scatter | solution.py:269
  729.0 522.9 %copy-start.1 = (bf16[512,1024]{1,0:T(8,128)(2,1)S(1)}, bf16[512,1024]{1,0:T(8,128)(2,1)}, u32[]{:S(2)}) copy-start(bf16[512,1024]{1,0:T(8,128)(2,1)} %param.19) | copy-start | bytes 3145732
Sparse Core Ops, SparseCore 0:
  29.3 44.4 all-gather.8
  83.2 11.9 reduce-scatter.15
  128.7 10.3 all-gather.10
  143.6 77.9 reduce-scatter.17
  223.0 46.9 all-gather.16
  272.1 44.4 all-gather.12
  318.8 14.4 reduce-scatter.23
  335.6 26.1 reduce-scatter.19
  371.3 21.1 all-gather.18
  406.7 77.9 reduce-scatter.25
  504.9 45.0 all-gather.20
  554.3 7.7 reduce-scatter.27
  636.3 13.3 all-gather.22
  651.7 14.8 all-gather.14
  668.7 77.9 reduce-scatter.29
  748.9 77.9 reduce-scatter.21
  830.3 86.7 reduce-scatter.43
  920.5 35.1 reduce-scatter.37
  959.4 86.3 reduce-scatter.39
  1049.2 86.3 reduce-scatter.41
  1139.1 35.1 reduce-scatter.31
  1177.9 35.1 reduce-scatter.33
  1216.6 35.1 reduce-scatter.35
where the time goes:
time: 1260 us
  waiting for transfers between devices  896 us (71%)
  matrix products  211 us (17%)
  blocking collectives  77.5 us (6%)
  other arithmetic  43.2 us (3%)
  between operations  15.6 us (1%)
    reduce_scatter x4, waiting for transfers between devices, sum_cols(): lax.psum_scatter(partial_sums, 'col', scatter_dimension=1, tiled=True)  223 us
    all_gather x4, waiting for transfers between devices, gather_cols(): return lax.all_gather(pieces, 'col', axis=1, tiled=True)  155 us
    reduce_scatter x1, waiting for transfers between devices, body(): lax.psum_scatter(grad_w_gate, 'dp', scatter_dimension=0, tiled=True)  90 us
    reduce_scatter x1, waiting for transfers between devices, body(): lax.psum_scatter(grad_w_up, 'dp', scatter_dimension=0, tiled=True)  89.8 us
    reduce_scatter x1, waiting for transfers between devices, body(): lax.psum_scatter(grad_w_down, 'dp', scatter_dimension=0, tiled=True)  87.1 us
    psum x4, blocking collectives, width_total(): return lax.psum(partial_sums, ('row', 'col'))  67.6 us
    all_gather x4, waiting for transfers between devices, gather_rows(): return lax.all_gather(pieces, 'row', axis=2, tiled=True)  51.9 us
    dot_general x7, matrix products, contract_rows(): jnp.einsum('ta,tb->ab', left, right, preferred_element_type=jnp.float32)  49.7 us
  transfers between devices with their start and end apart: 23, of which 22 were waited for; matrix products, arithmetic and copies ran while one was open for 9% of the time, Pallas kernels for 0%

commit v1 on v0

--- a/solution.py
+++ b/solution.py
@@ -21,7 +21,7 @@
 
 
 def sum_cols(partial_sums):
-    return lax.psum_scatter(partial_sums, "col", scatter_dimension=1, tiled=True)
+    return lax.psum_scatter(partial_sums.astype(jnp.bfloat16), "col", scatter_dimension=1, tiled=True).astype(jnp.float32)
 
 
 def gather_rows(pieces):
@@ -29,7 +29,11 @@
 
 
 def sum_rows(partial_sums):
-    return lax.psum_scatter(partial_sums, "row", scatter_dimension=2, tiled=True)
+    return lax.psum_scatter(partial_sums.astype(jnp.bfloat16), "row", scatter_dimension=2, tiled=True).astype(jnp.float32)
+
+
+def sum_dp(partial_sums):
+    return lax.psum_scatter(partial_sums.astype(jnp.bfloat16), "dp", scatter_dimension=0, tiled=True).astype(jnp.float32)
 
 
 def product(left, right):
@@ -264,13 +268,13 @@
     reduced = (
         lax.psum_scatter(grad_gain_attn, "dp", scatter_dimension=0, tiled=True),
         lax.psum_scatter(grad_gain_ffn, "dp", scatter_dimension=0, tiled=True),
-        lax.psum_scatter(grad_w_query, "dp", scatter_dimension=0, tiled=True),
-        lax.psum_scatter(grad_w_key, "dp", scatter_dimension=0, tiled=True),
-        lax.psum_scatter(grad_w_value, "dp", scatter_dimension=0, tiled=True),
-        lax.psum_scatter(grad_w_out, "dp", scatter_dimension=0, tiled=True),
-        lax.psum_scatter(grad_w_gate, "dp", scatter_dimension=0, tiled=True),
-        lax.psum_scatter(grad_w_up, "dp", scatter_dimension=0, tiled=True),
-        lax.psum_scatter(grad_w_down, "dp", scatter_dimension=0, tiled=True),
+        sum_dp(grad_w_query),
+        sum_dp(grad_w_key),
+        sum_dp(grad_w_value),
+        sum_dp(grad_w_out),
+        sum_dp(grad_w_gate),
+        sum_dp(grad_w_up),
+        sum_dp(grad_w_down),
     )
     gate_share, up_share = (reduced[6], reduced[7])
     return (

time: 1260 us -> 978 us (0.78)
  waiting for transfers between devices: 896 us -> 594 us
  other arithmetic: 43.2 us -> 64.3 us
    reduce_scatter x15, waiting for transfers between devices: 688 us -> 404 us  [the longest x7 226 us: sum_dp(): lax.psum_scatter(partial_sums.astype(jnp.bfloat16), 'dp', scatter_dimensi...]
    all_gather x4, waiting for transfers between devices: 51.9 us -> 31.5 us  [gather_rows(): return lax.all_gather(pieces, 'row', axis=2, tiled=True)]
    reshape x0 -> x7, other arithmetic: none -> 15.7 us  [as_blocks(): return matrix.reshape((1, 1) + matrix.shape)]
  transfers between devices with their start and end apart: 23 -> 23, of which waited for: 22 -> 21; matrix products, arithmetic and copies ran while one was open for 9% -> 20% of each run, Pallas kernels for 0% -> 0%
where the time goes in v1:
time: 978 us; the launch traced here: 974 us
  waiting for transfers between devices  594 us (61%)
  matrix products  209 us (21%)
  blocking collectives  75.1 us (8%)
  other arithmetic  64.3 us (7%)
  between operations  15.5 us (2%)
  local copies, waits for them, and re-layouts  13.4 us (1%)
    reduce_scatter x7, waiting for transfers between devices, sum_dp(): lax.psum_scatter(partial_sums.astype(jnp.bfloat16), 'dp', scatter_dimensi...  226 us
    all_gather x4, waiting for transfers between devices, gather_cols(): return lax.all_gather(pieces, 'col', axis=1, tiled=True)  156 us
    reduce_scatter x4, waiting for transfers between devices, sum_cols(): lax.psum_scatter(partial_sums.astype(jnp.bfloat16), 'col', scatter_dimens...  151 us
    psum x4, blocking collectives, width_total(): return lax.psum(partial_sums, ('row', 'col'))  65.2 us
    dot_general x7, matrix products, contract_rows(): jnp.einsum('ta,tb->ab', left, right, preferred_element_type=jnp.float32)  45.4 us
    dot_general x7, matrix products, product(): return jnp.dot(left, right, preferred_element_type=jnp.float32)  34.8 us
    dot_general x7, matrix products, times_transposed(): jnp.einsum('ta,ba->tb', left, right, preferred_element_type=jnp.float32)  33.8 us
    all_gather x4, waiting for transfers between devices, gather_rows(): return lax.all_gather(pieces, 'row', axis=2, tiled=True)  31.5 us
  transfers between devices with their start and end apart: 23, of which 21 were waited for; matrix products, arithmetic and copies ran while one was open for 20% of the time, Pallas kernels for 0%

profile of v1, /device:TPU:0, one launch (start us, length us, event | category | flops | bytes accessed | tf_op | source)
XLA Modules:
  0.0 973.5 jit_solution(7916494734413546643)
XLA Ops:
  8.6 18.5 %psum.28 = f32[1024]{0:T(1024)S(1)} all-reduce(f32[1024]{0:T(1024)S(1)} %fusion.113), channel_id=1, replica_groups=mesh['dp'=4,'row'=2,'col'=4] {'row','col'}, use_global_device_ids=true, to_apply=%region_1.0 | all-reduce | flops 1024 | bytes 8192 | tf_op jit(solution)/shard_map/psum | solution.py:16
  29.3 44.6 %all-gather.9.cloned.1.call-done = bf16[1024,1024]{1,0:T(8,128)(2,1)} async-done(((bf16[1024,256]{1,0:T(8,128)(2,1)}), bf16[1024,1024]{1,0:T(8,128)(2,1)}) %all-gather.9.cloned.1.call-update) | async-done | bytes 2097168 | tf_op jit(solution)/shard_map/all_gather | solution.py:20
  73.9 3.2 fusion.69
  84.4 6.6 reduce-scatter.16.cloned.1.call-done
  92.3 2.7 fusion.143
  96.5 2.5 copy.42
  101.5 9.8 %fusion.4 = f32[4,512,1024]{2,1,0:T(8,128)} fusion(pred[512,1024]{1,0:T(8,128)(4,1)} %get-tuple-element.92, bf16[1024,4,32]{0,2,1:T(8,128)(2,1)} %get-tuple-element.87, bf16[1024,4,32]{0,2,1:T(8,128)(2,1)} %get-tuple-element.88, bf16[1024,4,32]{0,2,1:T(8,128)(2,1)} %get-tuple-element.78, bf16[1024,4,32]{0,2,1:T(8,128)(2,1)} %get-tuple-element.77), kind=kOutput, calls=%fused_computation.5 | convolution fusion | flops 550505472 | bytes 9961472 | tf_op jit(solution)/shard_map/while/body/eval_jaxpr/reduce_sum | solution.py:119
  111.3 7.0 fusion.5
  118.3 4.9 fusion.98
  126.7 10.2 %all-gather.11.cloned.1.call-done = bf16[1,1024,512]{1,2,0:T(8,128)(2,1)} async-done(((bf16[1,1024,256]{1,2,0:T(8,128)(2,1)}), bf16[1,1024,512]{1,2,0:T(8,128)(2,1)}) %all-gather.11.cloned.1.call-update) | async-done | bytes 1048592 | tf_op jit(solution)/shard_map/all_gather | solution.py:28
  136.9 3.8 convolution_convert_fusion.2
  140.8 44.9 %reduce-scatter.18.cloned.1.call-done = bf16[1024,256]{1,0:T(8,128)(2,1)} async-done(((bf16[1024,1024]{1,0:T(8,128)(2,1)}), bf16[1024,256]{1,0:T(8,128)(2,1)}) %reduce-scatter.18.cloned.1.call-update) | async-done | bytes 524304 | tf_op jit(solution)/shard_map/reduce_scatter | solution.py:24
  187.0 15.2 %psum.29 = f32[1024]{0:T(1024)S(1)} all-reduce(f32[1024]{0:T(1024)S(1)} %multiply_reduce_fusion.2), channel_id=1, replica_groups=mesh['dp'=4,'row'=2,'col'=4] {'row','col'}, use_global_device_ids=true, to_apply=%region_7.8 | all-reduce | flops 1024 | bytes 8192 | tf_op jit(solution)/shard_map/psum | solution.py:16
  204.9 44.1 %all-gather.13.cloned.1.call-done = bf16[1024,1024]{1,0:T(8,128)(2,1)} async-done(((bf16[1024,256]{1,0:T(8,128)(2,1)}), bf16[1024,1024]{1,0:T(8,128)(2,1)}) %all-gather.13.cloned.1.call-update) | async-done | bytes 2097168 | tf_op jit(solution)/shard_map/all_gather | solution.py:20
  249.0 9.4 convert_bitcast_fusion.1
  258.5 6.1 convert_bitcast_fusion.2
  264.6 7.5 pad_maximum_fusion
  272.2 22.7 %all-gather.17.cloned.1.call-done = bf16[1024,1024]{1,0:T(8,128)(2,1)} async-done(((bf16[1024,256]{1,0:T(8,128)(2,1)}), bf16[1024,1024]{1,0:T(8,128)(2,1)}) %all-gather.17.cloned.1.call-update) | async-done | bytes 2097168 | tf_op jit(solution)/shard_map/all_gather | solution.py:20
  294.9 9.6 convert_bitcast_fusion
  305.0 6.7 reduce-scatter.20.cloned.1.call-done
  311.6 6.5 convert_element_type.203
  318.1 9.0 reduce-scatter.24.cloned.1.call-done
  327.1 6.3 fusion.20
  335.8 21.2 %all-gather.19.cloned.1.call-done = bf16[2,1024,2048]{2,1,0:T(8,128)(2,1)} async-done(((bf16[2,1024,1024]{2,1,0:T(8,128)(2,1)}), bf16[2,1024,2048]{2,1,0:T(8,128)(2,1)}) %all-gather.19.cloned.1.call-update) | async-done | bytes 8388624 | tf_op jit(solution)/shard_map/all_gather | solution.py:28
  357.1 7.9 fusion.48
  365.1 5.7 add_convert_fusion.1
  370.9 44.9 %reduce-scatter.26.cloned.1.call-done = bf16[1024,256]{1,0:T(8,128)(2,1)} async-done(((bf16[1024,1024]{1,0:T(8,128)(2,1)}), bf16[1024,256]{1,0:T(8,128)(2,1)}) %reduce-scatter.26.cloned.1.call-update) | async-done | bytes 524304 | tf_op jit(solution)/shard_map/reduce_scatter | solution.py:24
  417.4 15.2 %psum.30 = f32[1024]{0:T(1024)S(1)} all-reduce(f32[1024]{0:T(1024)S(1)} %get-tuple-element.53), channel_id=1, replica_groups=mesh['dp'=4,'row'=2,'col'=4] {'row','col'}, use_global_device_ids=true, to_apply=%region_13.14 | all-reduce | flops 1024 | bytes 8192 | tf_op jit(solution)/shard_map/psum | solution.py:16
  435.0 44.7 %all-gather.21.cloned.1.call-done = bf16[1024,1024]{1,0:T(8,128)(2,1)} async-done(((bf16[1024,256]{1,0:T(8,128)(2,1)}), bf16[1024,1024]{1,0:T(8,128)(2,1)}) %all-gather.21.cloned.1.call-update) | async-done | bytes 2097168 | tf_op jit(solution)/shard_map/all_gather | solution.py:20
  479.7 3.8 fusion.70
  484.5 5.8 reduce-scatter.28.cloned.1.call-done
  491.7 4.5 fusion.146
  496.2 15.5 %fusion.89 = f32[512,4,64]{0,2,1:T(8,128)} fusion(f32[4,512,1024]{2,1,0:T(8,128)} %fusion.5, f32[4,512,1024]{2,1,0:T(8,128)} %fusion.146, bf16[1024,4,32]{0,2,1:T(8,128)(2,1)S(1)} %copy-done.21, bf16[1024,4,32]{0,2,1:T(8,128)(2,1)S(1)} %copy-done.19), kind=kOutput, calls=%fused_computation.103 | convolution fusion | flops 279972864 | bytes 17825792 | tf_op jit(solution)/shard_map/while/body/eval_jaxpr/hqk,khd->qhd/dot_general | solution.py:147
  511.7 4.5 fusion.147
  516.3 13.5 %fusion.86 = f32[512,4,64]{0,2,1:T(8,128)} fusion(f32[4,512,1024]{2,1,0:T(8,128)} %fusion.4, f32[4,512,1024]{2,1,0:T(8,128)} %fusion.147, bf16[1024,4,32]{0,2,1:T(8,128)(2,1)S(1)} %copy-done.21, bf16[1024,4,32]{0,2,1:T(8,128)(2,1)S(1)} %copy-done.19), kind=kOutput, calls=%fused_computation.102 | convolution fusion | flops 279972864 | bytes 17825792 | tf_op jit(solution)/shard_map/while/body/eval_jaxpr/hqk,khd->qhd/dot_general | solution.py:147
  529.7 12.6 %fusion.34 = f32[4,64,1024]{2,1,0:T(8,128)} fusion(f32[4,512,1024]{2,1,0:T(8,128)} %fusion.5, f32[4,512,1024]{2,1,0:T(8,128)} %fusion.146, bf16[1024,4,32]{0,2,1:T(8,128)(2,1)S(1)} %copy-done.17, bf16[1024,4,32]{0,2,1:T(8,128)(2,1)S(1)} %copy-done.15), kind=kOutput, calls=%fused_computation.48 | convolution fusion | flops 279448576 | bytes 35127296 | tf_op jit(solution)/shard_map/while/body/eval_jaxpr/hqk,qhd->khd/dot_general | solution.py:149
  542.4 12.8 %fusion.77 = f32[1024,4,64]{0,2,1:T(8,128)S(1)} fusion(f32[4,64,1024]{2,1,0:T(8,128)} %fusion.34, f32[4,512,1024]{2,1,0:T(8,128)} %fusion.4, f32[4,512,1024]{2,1,0:T(8,128)} %fusion.147, bf16[1024,4,32]{0,2,1:T(8,128)(2,1)S(1)} %copy-done.15, bf16[1024,4,32]{0,2,1:T(8,128)(2,1)} %get-tuple-element.88), kind=kOutput, calls=%fused_computation.97 | convolution fusion | flops 279710720 | bytes 19398656 | tf_op jit(solution)/shard_map/while/body/eval_jaxpr/hqk,qhd->khd/dot_general | solution.py:149
  557.1 4.3 fusion.50
  561.4 4.2 fusion.80
  567.2 9.5 fusion.45
  576.8 9.9 %convolution_convert_fusion = bf16[1024,2048]{1,0:T(8,128)(2,1)} fusion(bf16[1024,1024]{1,0:T(8,128)(2,1)} %all-gather.13.cloned.1.call-done, bf16[2,1024,2048]{2,1,0:T(8,128)(2,1)} %all-gather.19.cloned.1.call-done), kind=kOutput, calls=%fused_computation.53 | convolution fusion | flops 4297064448 | bytes 10485760 | tf_op jit(solution)/shard_map/ta,tb->ab/dot_general | solution.py:44
  587.1 9.4 convolution_convert_fusion.1
  597.8 3.8 convolution_convert_fusion.3
  601.8 4.3 convolution_convert_fusion.4
  606.2 4.1 convolution_convert_fusion.5
  610.4 4.3 convolution_convert_fusion.6
  615.0 2.7 fusion.121
  619.0 2.7 add_convert_fusion
  621.8 9.6 fusion.60
  632.7 4.3 reduce-scatter.44.cloned.1.call-done
  637.0 2.8 bitcast_convert_fusion
  639.8 52.7 %reduce-scatter.42.cloned.1.call-done = bf16[256,2048]{1,0:T(8,128)(2,1)} async-done(((bf16[1024,2048]{1,0:T(8,128)(2,1)}), bf16[256,2048]{1,0:T(8,128)(2,1)}) %reduce-scatter.42.cloned.1.call-update) | async-done | bytes 1048592 | tf_op jit(solution)/shard_map/reduce_scatter | solution.py:36
  692.4 2.8 bitcast_convert_fusion.1
  695.2 52.7 %reduce-scatter.40.cloned.1.call-done = bf16[256,2048]{1,0:T(8,128)(2,1)} async-done(((bf16[1024,2048]{1,0:T(8,128)(2,1)}), bf16[256,2048]{1,0:T(8,128)(2,1)}) %reduce-scatter.40.cloned.1.call-update) | async-done | bytes 1048592 | tf_op jit(solution)/shard_map/reduce_scatter | solution.py:36
  747.9 2.8 bitcast_convert_fusion.2
  750.7 27.9 %reduce-scatter.38.cloned.1.call-done = bf16[128,1024]{1,0:T(8,128)(2,1)} async-done(((bf16[512,1024]{1,0:T(8,128)(2,1)}), bf16[128,1024]{1,0:T(8,128)(2,1)}) %reduce-scatter.38.cloned.1.call-update) | async-done | bytes 262160 | tf_op jit(solution)/shard_map/reduce_scatter | solution.py:36
  780.5 29.0 %reduce-scatter.36.cloned.1.call-done = bf16[256,512]{1,0:T(8,128)(2,1)} async-done(((bf16[1024,512]{1,0:T(8,128)(2,1)}), bf16[256,512]{1,0:T(8,128)(2,1)}) %reduce-scatter.36.cloned.1.call-update) | async-done | bytes 262160 | tf_op jit(solution)/shard_map/reduce_scatter | solution.py:36
  811.3 29.4 %reduce-scatter.34.cloned.1.call-done = bf16[256,512]{1,0:T(8,128)(2,1)} async-done(((bf16[1024,512]{1,0:T(8,128)(2,1)}), bf16[256,512]{1,0:T(8,128)(2,1)}) %reduce-scatter.34.cloned.1.call-update) | async-done | bytes 262160 | tf_op jit(solution)/shard_map/reduce_scatter | solution.py:36
  842.5 29.6 %reduce-scatter.32.cloned.1.call-done = bf16[256,512]{1,0:T(8,128)(2,1)} async-done(((bf16[1024,512]{1,0:T(8,128)(2,1)}), bf16[256,512]{1,0:T(8,128)(2,1)}) %reduce-scatter.32.cloned.1.call-update) | async-done | bytes 262160 | tf_op jit(solution)/shard_map/reduce_scatter | solution.py:36
  874.0 44.2 %reduce-scatter.30.cloned.1.call-done = bf16[1024,256]{1,0:T(8,128)(2,1)} async-done(((bf16[1024,1024]{1,0:T(8,128)(2,1)}), bf16[1024,256]{1,0:T(8,128)(2,1)}) %reduce-scatter.30.cloned.1.call-update) | async-done | bytes 524304 | tf_op jit(solution)/shard_map/reduce_scatter | solution.py:24
  919.7 9.9 %all-reduce.2 = (f32[256]{0:T(256)S(1)}, f32[256]{0:T(256)S(1)}) all-reduce(f32[256]{0:T(256)S(1)} %get-tuple-element.54, f32[256]{0:T(256)S(1)} %get-tuple-element.52), channel_id=10, replica_groups=mesh['dp'=4,'row'=2,'col'=4] {'dp'}, use_global_device_ids=true, to_apply=%region_21.22.clone | all-reduce | flops 512 | bytes 4096
  929.6 16.3 %psum.31 = f32[1024]{0:T(1024)S(1)} all-reduce(f32[1024]{0:T(1024)S(1)} %get-tuple-element.55), channel_id=1, replica_groups=mesh['dp'=4,'row'=2,'col'=4] {'row','col'}, use_global_device_ids=true, to_apply=%region_19.20 | all-reduce | flops 1024 | bytes 8192 | tf_op jit(solution)/shard_map/psum | solution.py:16
  947.1 16.8 %reduce-scatter.22.cloned.1.call-done = bf16[1024,256]{1,0:T(8,128)(2,1)} async-done(((bf16[1024,1024]{1,0:T(8,128)(2,1)}), bf16[1024,256]{1,0:T(8,128)(2,1)}) %reduce-scatter.22.cloned.1.call-update) | async-done | bytes 524304 | tf_op jit(solution)/shard_map/reduce_scatter | solution.py:24
  963.9 2.9 fusion.105
  (167 shorter events, 50.4 us)
Async XLA Ops:
  7.2 129.7 %copy-start = (bf16[512,1024]{1,0:T(8,128)(2,1)S(1)}, bf16[512,1024]{1,0:T(8,128)(2,1)}, u32[]{:S(2)}) copy-start(bf16[512,1024]{1,0:T(8,128)(2,1)} %param.19) | copy-start | bytes 3145732
  7.2 66.7 %all-gather.9.cloned.1.call-start = ((), (), s32[]{:S(2)}) async-start(), calls=%async_computation.15 | async-start | bytes 2621440 | tf_op jit(solution)/shard_map/all_gather | solution.py:20
  27.1 50.0 %copy-start.22 = (f32[1024]{0:T(1024)}, f32[1024]{0:T(1024)S(1)}, u32[]{:S(2)}) copy-start(f32[1024]{0:T(1024)S(1)} %add_rsqrt_fusion.1) | copy-start | bytes 12292
  29.2 47.9 %copy-start.33 = (bf16[1024,512]{1,0:T(8,128)(2,1)S(1)}, bf16[1024,512]{1,0:T(8,128)(2,1)}, u32[]{:S(2)}) copy-start(bf16[1024,512]{1,0:T(8,128)(2,1)} %param.17) | copy-start | bytes 3145732
  29.2 61.8 %reduce-scatter.16.cloned.1.call-start = ((), (), s32[]{:S(2)}) async-start(), calls=%async_computation.16 | async-start | bytes 4718592 | tf_op jit(solution)/shard_map/reduce_scatter | solution.py:32
  73.9 3.3 copy-start.31
  77.2 1.3 copy-start.35
  79.7 2.2 copy-start.27
  79.7 2.3 copy-start.24
  81.7 55.2 %all-gather.11.cloned.1.call-start = ((), (), s32[]{:S(2)}) async-start(), calls=%async_computation.17 | async-start | bytes 1572864 | tf_op jit(solution)/shard_map/all_gather | solution.py:28
  82.5 16.5 %copy-start.9 = (f32[1024,32]{0,1:T(8,128)}, f32[1024,32]{0,1:T(8,128)S(1)}, u32[]{:S(2)}) copy-start(f32[1024,32]{0,1:T(8,128)S(1)} %get-tuple-element.90) | copy-start | bytes 393220
  101.5 9.8 %copy-start.12 = (pred[512,1024]{1,0:T(8,128)(4,1)S(1)}, pred[512,1024]{1,0:T(8,128)(4,1)}, u32[]{:S(2)}) copy-start(pred[512,1024]{1,0:T(8,128)(4,1)} %get-tuple-element.91) | copy-start | bytes 1572868
  101.5 9.8 %copy-start.14 = (bf16[1024,4,32]{0,2,1:T(8,128)(2,1)S(1)}, bf16[1024,4,32]{0,2,1:T(8,128)(2,1)}, u32[]{:S(2)}) copy-start(bf16[1024,4,32]{0,2,1:T(8,128)(2,1)} %get-tuple-element.87) | copy-start | bytes 786436
  101.5 9.8 %copy-start.16 = (bf16[1024,4,32]{0,2,1:T(8,128)(2,1)S(1)}, bf16[1024,4,32]{0,2,1:T(8,128)(2,1)}, u32[]{:S(2)}) copy-start(bf16[1024,4,32]{0,2,1:T(8,128)(2,1)} %get-tuple-element.88) | copy-start | bytes 786436
  101.5 9.8 %copy-start.18 = (bf16[1024,4,32]{0,2,1:T(8,128)(2,1)S(1)}, bf16[1024,4,32]{0,2,1:T(8,128)(2,1)}, u32[]{:S(2)}) copy-start(bf16[1024,4,32]{0,2,1:T(8,128)(2,1)} %get-tuple-element.77) | copy-start | bytes 786436
  101.5 9.8 %copy-start.20 = (bf16[1024,4,32]{0,2,1:T(8,128)(2,1)S(1)}, bf16[1024,4,32]{0,2,1:T(8,128)(2,1)}, u32[]{:S(2)}) copy-start(bf16[1024,4,32]{0,2,1:T(8,128)(2,1)} %get-tuple-element.78) | copy-start | bytes 786436
  118.3 5.8 copy-start.3
  126.4 59.3 %copy-start.2 = (bf16[1024,256]{1,0:T(8,128)(2,1)S(1)}, bf16[1024,256]{1,0:T(8,128)(2,1)}, u32[]{:S(2)}) copy-start(bf16[1024,256]{1,0:T(8,128)(2,1)} %param.13) | copy-start | bytes 1572868
  126.4 75.8 %copy-start.25 = (f32[256]{0:T(256)S(1)}, f32[256]{0:T(256)}, u32[]{:S(2)}) copy-start(f32[256]{0:T(256)} %param.15) | copy-start | bytes 3076
  126.4 59.3 %reduce-scatter.18.cloned.1.call-start = ((), (), s32[]{:S(2)}) async-start(), calls=%async_computation.18 | async-start | bytes 2621440 | tf_op jit(solution)/shard_map/reduce_scatter | solution.py:24
  140.7 108.3 %all-gather.13.cloned.1.call-start = ((), (), s32[]{:S(2)}) async-start(), calls=%async_computation.19 | async-start | bytes 2621440 | tf_op jit(solution)/shard_map/all_gather | solution.py:20
  204.3 90.6 %all-gather.17.cloned.1.call-start = ((), (), s32[]{:S(2)}) async-start(), calls=%async_computation.23 | async-start | bytes 2621440 | tf_op jit(solution)/shard_map/all_gather | solution.py:20
  204.8 106.8 %reduce-scatter.20.cloned.1.call-start = ((), (), s32[]{:S(2)}) async-start(), calls=%async_computation.20 | async-start | bytes 12582912 | tf_op jit(solution)/shard_map/reduce_scatter | solution.py:32
  249.0 9.5 copy-start.29
  249.0 9.5 copy-start.32
  272.1 55.0 %reduce-scatter.24.cloned.1.call-start = ((), (), s32[]{:S(2)}) async-start(), calls=%async_computation.24 | async-start | bytes 6291456 | tf_op jit(solution)/shard_map/reduce_scatter | solution.py:32
  304.5 52.5 %all-gather.19.cloned.1.call-start = ((), (), s32[]{:S(2)}) async-start(), calls=%async_computation.25 | async-start | bytes 12582912 | tf_op jit(solution)/shard_map/all_gather | solution.py:28
  335.8 80.0 %reduce-scatter.26.cloned.1.call-start = ((), (), s32[]{:S(2)}) async-start(), calls=%async_computation.26 | async-start | bytes 2621440 | tf_op jit(solution)/shard_map/reduce_scatter | solution.py:24
  357.1 8.0 copy-start.28
  357.1 8.0 copy-start.30
  365.0 50.7 %copy-start.4 = (bf16[1024,256]{1,0:T(8,128)(2,1)S(1)}, bf16[1024,256]{1,0:T(8,128)(2,1)}, u32[]{:S(2)}) copy-start(bf16[1024,256]{1,0:T(8,128)(2,1)} %reduce-scatter.18.cloned.1.call-done) | copy-start | bytes 1572868
  365.1 67.5 %copy-start.5 = (bf16[1024,256]{1,0:T(8,128)(2,1)S(1)}, bf16[1024,256]{1,0:T(8,128)(2,1)}, u32[]{:S(2)}) copy-start(bf16[1024,256]{1,0:T(8,128)(2,1)} %param.23) | copy-start | bytes 1572868
  370.8 108.8 %all-gather.21.cloned.1.call-start = ((), (), s32[]{:S(2)}) async-start(), calls=%async_computation.27 | async-start | bytes 2621440 | tf_op jit(solution)/shard_map/all_gather | solution.py:20
  434.9 55.4 %reduce-scatter.28.cloned.1.call-start = ((), (), s32[]{:S(2)}) async-start(), calls=%async_computation.28 | async-start | bytes 1572864 | tf_op jit(solution)/shard_map/reduce_scatter | solution.py:32
  483.5 83.7 %all-gather.15.cloned.1.call-start = ((), (), s32[]{:S(2)}) async-start(), calls=%async_computation.21 | async-start | bytes 6291456 | tf_op jit(solution)/shard_map/all_gather | solution.py:28
  484.3 117.5 %all-gather.23.cloned.1.call-start = ((), (), s32[]{:S(2)}) async-start(), calls=%async_computation.29 | async-start | bytes 4718592 | tf_op jit(solution)/shard_map/all_gather | solution.py:28
  491.6 20.1 %copy-start.7 = (bf16[1,512,256]{1,2,0:T(8,128)(2,1)}, bf16[1,512,256]{1,2,0:T(8,128)(2,1)S(1)}, u32[]{:S(2)}) copy-start(bf16[1,512,256]{1,2,0:T(8,128)(2,1)S(1)} %copy.45) | copy-start | bytes 786436
  491.6 4.6 copy-start.19
  491.6 4.5 copy-start.21
  516.3 13.5 %copy-start.15 = (bf16[1024,4,32]{0,2,1:T(8,128)(2,1)S(1)}, bf16[1024,4,32]{0,2,1:T(8,128)(2,1)}, u32[]{:S(2)}) copy-start(bf16[1024,4,32]{0,2,1:T(8,128)(2,1)} %get-tuple-element.87) | copy-start | bytes 786436
  516.3 13.5 %copy-start.17 = (bf16[1024,4,32]{0,2,1:T(8,128)(2,1)S(1)}, bf16[1024,4,32]{0,2,1:T(8,128)(2,1)}, u32[]{:S(2)}) copy-start(bf16[1024,4,32]{0,2,1:T(8,128)(2,1)} %get-tuple-element.88) | copy-start | bytes 786436
  542.4 12.8 %copy-start.10 = (f32[1024,32]{0,1:T(8,128)S(1)}, f32[1024,32]{0,1:T(8,128)}, u32[]{:S(2)}) copy-start(f32[1024,32]{0,1:T(8,128)} %copy-done.9) | copy-start | bytes 393220
  555.2 1.9 copy-start.8
  566.9 70.1 %reduce-scatter.44.cloned.1.call-start = ((), (), s32[]{:S(2)}) async-start(), calls=%async_computation.37 | async-start | bytes 5242880 | tf_op jit(solution)/shard_map/reduce_scatter | solution.py:36
  576.7 115.7 %reduce-scatter.42.cloned.1.call-start = ((), (), s32[]{:S(2)}) async-start(), calls=%async_computation.36 | async-start | bytes 5242880 | tf_op jit(solution)/shard_map/reduce_scatter | solution.py:36
  586.7 161.2 %reduce-scatter.40.cloned.1.call-start = ((), (), s32[]{:S(2)}) async-start(), calls=%async_computation.35 | async-start | bytes 5242880 | tf_op jit(solution)/shard_map/reduce_scatter | solution.py:36
  596.5 1.3 copy-start.37
  596.6 182.1 %reduce-scatter.38.cloned.1.call-start = ((), (), s32[]{:S(2)}) async-start(), calls=%async_computation.34 | async-start | bytes 1310720 | tf_op jit(solution)/shard_map/reduce_scatter | solution.py:36
  601.7 207.8 %reduce-scatter.36.cloned.1.call-start = ((), (), s32[]{:S(2)}) async-start(), calls=%async_computation.33 | async-start | bytes 1310720 | tf_op jit(solution)/shard_map/reduce_scatter | solution.py:36
  606.1 234.6 %reduce-scatter.34.cloned.1.call-start = ((), (), s32[]{:S(2)}) async-start(), calls=%async_computation.32 | async-start | bytes 1310720 | tf_op jit(solution)/shard_map/reduce_scatter | solution.py:36
  610.3 4.6 copy-start.34
  610.4 261.8 %reduce-scatter.32.cloned.1.call-start = ((), (), s32[]{:S(2)}) async-start(), calls=%async_computation.31 | async-start | bytes 1310720 | tf_op jit(solution)/shard_map/reduce_scatter | solution.py:36
  614.7 303.4 %reduce-scatter.30.cloned.1.call-start = ((), (), s32[]{:S(2)}) async-start(), calls=%async_computation.30 | async-start | bytes 2621440 | tf_op jit(solution)/shard_map/reduce_scatter | solution.py:24
  615.0 2.7 copy-start.13
  615.0 2.7 copy-start.36
  617.7 1.3 copy-start.11
  621.7 9.7 copy-start.38
  621.7 342.2 %reduce-scatter.22.cloned.1.call-start = ((), (), s32[]{:S(2)}) async-start(), calls=%async_computation.22 | async-start | bytes 2621440 | tf_op jit(solution)/shard_map/reduce_scatter | solution.py:24
  639.8 278.4 %copy-start.23 = (f32[1024]{0:T(1024)S(1)}, f32[1024]{0:T(1024)}, u32[]{:S(2)}) copy-start(f32[1024]{0:T(1024)} %copy-done.22) | copy-start | bytes 12292
  639.8 278.4 %copy-start.26 = (f32[256]{0:T(256)S(1)}, f32[256]{0:T(256)}, u32[]{:S(2)}) copy-start(f32[256]{0:T(256)} %param.14) | copy-start | bytes 3076
  695.2 268.7 %copy-start.6 = (bf16[1024,256]{1,0:T(8,128)(2,1)S(1)}, bf16[1024,256]{1,0:T(8,128)(2,1)}, u32[]{:S(2)}) copy-start(bf16[1024,256]{1,0:T(8,128)(2,1)} %reduce-scatter.26.cloned.1.call-done) | copy-start | bytes 1572868
  778.6 188.2 %copy-start.1 = (bf16[512,1024]{1,0:T(8,128)(2,1)S(1)}, bf16[512,1024]{1,0:T(8,128)(2,1)}, u32[]{:S(2)}) copy-start(bf16[512,1024]{1,0:T(8,128)(2,1)} %param.19) | copy-start | bytes 3145732
Sparse Core Ops, SparseCore 0:
  29.3 44.4 all-gather.8
  81.8 9.0 reduce-scatter.15
  126.5 10.3 all-gather.10
  140.9 44.7 reduce-scatter.17
  204.4 44.5 all-gather.12
  250.4 44.4 all-gather.16
  297.2 14.3 reduce-scatter.19
  313.9 13.1 reduce-scatter.23
  335.9 21.1 all-gather.18
  370.9 44.7 reduce-scatter.25
  435.0 44.5 all-gather.20
  483.6 6.5 reduce-scatter.27
  492.4 14.8 all-gather.14
  567.0 13.2 all-gather.22
  583.2 53.7 reduce-scatter.43
  639.8 52.5 reduce-scatter.41
  695.3 52.5 reduce-scatter.39
  750.6 27.9 reduce-scatter.37
  781.5 27.9 reduce-scatter.35
  812.8 27.8 reduce-scatter.33
  844.2 27.9 reduce-scatter.31
  874.5 43.6 reduce-scatter.29
  920.4 43.4 reduce-scatter.21
